TPU v7x, 128 devices: a whole 4x4x4 slice. The times are simulated.
128 devices in a mesh: row: 8 (over x, y_lo), col: 16 (over y_hi, z, core).
Axes of the slice: x: 4, y: 4 (y_hi: 2, y_lo: 2; y = y_hi * 2 + y_lo), z: 4, core: 2. Of those that a mesh axis runs over, the one named last changes fastest.
Arguments:
- objects: float32 [4, 4096, 8192], P(None, 'row', 'col'), may hold values from -5 to 5
- illumination: float32 [2, 256, 256], replicated, may hold values from -5 to 5
- propagator_phase: float32 [256, 256], replicated, may hold values from -3.140625 to 3.140625
- intensity: bfloat16 [1536, 256, 256], P(('row', 'col')), may hold values from 0 to 2
- offsets: int32 [1536, 2], P(('row', 'col')), may hold values from -1 to 3, as said below
- counts: int32 [128], P(('row', 'col')), may hold values from 0 to 12, as said below
Outputs:
- gradient: float32 [4, 4096, 8192], P(None, 'row', 'col')
Inputs may be any that keep to these rules, and one draw needn't show every extreme that they name: `counts`: for every device, its count plus the count of the device 16 // 2 further along col (cyclically, same row) is at most 12; some device has exactly 12; every device at row index 0 has a live slot. `offsets`: the first slot of every device has column offset 512 // 128 - 1.
All inputs are finite; a program needn't handle non-finite values.
Results may differ from a plain program's by a relative error of at most 0.015.
Values may be sent and summed in bfloat16 or wider, within the bound.
A program may use at most 128 MiB of HBM per device.

v0:
```python
import math

import jax
import jax.numpy as jnp
import numpy as np
from jax import lax
from jax.experimental import pallas as pl
from jax.experimental.pallas import tpu as pltpu
from jax.sharding import PartitionSpec as P

EXTENT = 256
HALF = EXTENT // 2
MESH = pl.DeviceIdType.MESH


def tables(extent):
    half = extent // 2
    number = np.arange(extent, dtype=np.int32)
    turns = number[:, None] * number[None, :] % extent
    angle = turns.astype(np.float32) * np.float32(2.0 * math.pi / extent)
    scale = np.float32(1.0 / math.sqrt(extent))
    cosine = (np.cos(angle) * scale).astype(jnp.bfloat16)
    sine = (np.sin(angle) * scale).astype(jnp.bfloat16)
    folded = np.concatenate([cosine[:, : half + 1], sine[:, 1:half]], axis=1)
    order = np.concatenate([number[: half + 1], extent - number[1:half]])
    pick = np.eye(extent, dtype=np.float32)[order].astype(jnp.bfloat16)
    return tuple(jnp.asarray(np.ascontiguousarray(x)) for x in (folded, folded.T, pick, pick.T))


def product(a, b):
    return jnp.dot(a, b, preferred_element_type=jnp.float32)


def half(x):
    return x.astype(jnp.bfloat16)


class Place:
    def __init__(self):
        r, c = lax.axis_index("row"), lax.axis_index("col")
        self.has_above, self.has_below = r > 0, r < lax.axis_size("row") - 1
        self.has_left, self.has_right = c > 0, c < lax.axis_size("col") - 1
        self.above, self.below = (r - 1, c), (r + 1, c)
        self.left, self.right = (r, c - 1), (r, c + 1)
        self.sides = (
            (self.has_above, self.above),
            (self.has_below, self.below),
            (self.has_left, self.left),
            (self.has_right, self.right),
        )

    def greet(self):
        barrier = pltpu.get_barrier_semaphore()
        for there, device in self.sides:
            @pl.when(there)
            def _(device=device):
                pl.semaphore_signal(barrier, inc=1, device_id=device, device_id_type=MESH)

        pl.semaphore_wait(barrier, sum(there.astype(jnp.int32) for there, _ in self.sides))


class Sends:
    def __init__(self, send, recv):
        self.send, self.recv, self.all = send, recv, {}

    def add(self, key, source, target, device, sent, received):
        k = len(self.all)
        copy = pltpu.make_async_remote_copy(
            src_ref=source, dst_ref=target, send_sem=self.send.at[k], recv_sem=self.recv.at[k],
            device_id=device, device_id_type=MESH,
        )
        self.all[key] = (copy, sent, received)

    def start(self, *keys):
        for key in keys:
            copy, sent, _ = self.all[key]
            pl.when(sent)(copy.start)

    def wait_recv(self, *keys):
        for key in keys:
            copy, _, received = self.all[key]
            pl.when(received)(copy.wait_recv)

    def wait_send(self):
        for copy, sent, _ in self.all.values():
            pl.when(sent)(copy.wait_send)


def both(a, b):
    return jnp.logical_and(a, b)


def halo_kernel(
    objects, phase, pick, pick_t, ext, spread, acc, stage, angle, order, loads, send, recv
):
    tile = objects.shape[1]
    near, far, end = HALF, HALF + tile, 2 * HALF + tile
    own = slice(near, far)
    first, last = slice(0, near), slice(far, end)
    top, bottom = slice(near, 2 * near), slice(tile, far)
    place = Place()
    bands = ((tile - HALF, HALF), (0, HALF), (HALF, tile - 2 * HALF))
    loading = [
        pltpu.make_async_copy(objects.at[:, pl.ds(at, size)], stage.at[:, pl.ds(at, size)], loads.at[k])
        for k, (at, size) in enumerate(bands)
    ]
    parameters = [
        pltpu.make_async_copy(source, target, loads.at[3 + k])
        for k, (source, target) in enumerate(
            ((phase, angle), (pick, order.at[0]), (pick_t, order.at[1]))
        )
    ]
    for copy in loading + parameters:
        copy.start()
    place.greet()

    sends = Sends(send, recv)

    def route(key, source, target, device, sent, received):
        sends.add(key, ext.at[(slice(None),) + source], ext.at[(slice(None),) + target], device, sent, received)

    middle = slice(2 * near, tile)
    for name, cols in (("l", top), ("r", bottom), ("m", middle)):
        route("down" + name, (bottom, cols), (first, cols), place.below, place.has_below, place.has_above)
        route("up" + name, (top, cols), (last, cols), place.above, place.has_above, place.has_below)
    for k, (at, size) in enumerate(bands):
        rows = slice(near + at, near + at + size)
        route(f"right{k}", (rows, bottom), (rows, first), place.right, place.has_right, place.has_left)
        route(f"left{k}", (rows, top), (rows, last), place.left, place.has_left, place.has_right)
    for name, rows, there in (("t", first, place.has_above), ("b", last, place.has_below)):
        route("right" + name, (rows, bottom), (rows, first), place.right,
              both(place.has_right, there), both(place.has_left, there))
        route("left" + name, (rows, top), (rows, last), place.left,
              both(place.has_left, there), both(place.has_right, there))

    def cast(k):
        loading[k].wait()
        at, size = bands[k]
        for plane in range(4):
            ext[plane, near + at:near + at + size, near:far] = stage[plane, at:at + size].astype(jnp.bfloat16)

    cast(0)
    sends.start("downl", "downr", "right0", "left0")
    cast(1)
    sends.start("upl", "upr", "right1", "left1")
    cast(2)
    sends.start("right2", "left2", "downm", "upm")

    def blank(there, rows, cols):
        @pl.when(jnp.logical_not(there))
        def _():
            part = ext.at[:, rows, cols]
            part[...] = jnp.zeros(part.shape, jnp.bfloat16)

    blank(place.has_above, first, own)
    blank(place.has_below, last, own)
    blank(place.has_left, own, first)
    blank(place.has_right, own, last)
    for rows, there in ((first, place.has_above), (last, place.has_below)):
        blank(both(there, place.has_left), rows, first)
        blank(both(there, place.has_right), rows, last)
    for copy in parameters:
        copy.wait()
    rest, ordered = angle[...], 0.0
    for _ in range(3):
        part = half(rest)
        rest = rest - part.astype(jnp.float32)
        ordered = ordered + product(half(product(order[0], part)), order[1])
    spread[0] = jnp.cos(ordered)
    spread[1] = jnp.sin(ordered)
    for plane in range(4):
        acc[plane] = jnp.zeros(acc.shape[1:], jnp.float32)

    sends.wait_recv("downl", "downr")
    sends.start("leftt", "rightt")
    sends.wait_recv("upl", "upr")
    sends.start("leftb", "rightb")
    sends.wait_recv(*(f"{side}{k}" for side in ("right", "left") for k in range(3)))
    sends.wait_recv("downm", "upm", "leftt", "rightt", "leftb", "rightb")
    sends.wait_send()


def halo(objects, phase, pick, pick_t):
    tile = objects.shape[1]
    size = tile + 2 * HALF
    vmem = pl.BlockSpec(memory_space=pltpu.VMEM)
    return pl.pallas_call(
        halo_kernel,
        out_shape=(
            pltpu.VMEM((4, size, size), jnp.bfloat16),
            pltpu.VMEM((2, EXTENT, EXTENT), jnp.float32),
            pltpu.VMEM((4, size, size), jnp.float32),
        ),
        in_specs=[pl.BlockSpec(memory_space=pltpu.HBM)] * 4,
        out_specs=(vmem, vmem, vmem),
        scratch_shapes=[
            pltpu.VMEM(objects.shape, jnp.float32),
            pltpu.VMEM((EXTENT, EXTENT), jnp.float32),
            pltpu.VMEM((2, EXTENT, EXTENT), jnp.bfloat16),
            pltpu.SemaphoreType.DMA((6,)),
            pltpu.SemaphoreType.DMA((16,)),
            pltpu.SemaphoreType.DMA((16,)),
        ],
        compiler_params=pltpu.CompilerParams(
            collective_id=0, has_side_effects=True, vmem_limit_bytes=24 * 2**20
        ),
    )(*(pltpu.with_memory_space_constraint(x, pltpu.HBM) for x in (objects, phase, pick, pick_t)))


def margin_kernel(
    acc, out, row_send, row_recv, col_send, col_recv, corner_send, corner_recv, send, recv
):
    tile = out.shape[1]
    near, far, end = HALF, HALF + tile, 2 * HALF + tile
    own = slice(near, far)
    edges = (slice(0, near), slice(far, end))
    inner = slice(near, tile - near)
    outer = (slice(0, near), slice(tile - near, tile))
    place = Place()
    place.greet()
    rows = ((place.has_above, place.above), (place.has_below, place.below))
    cols = ((place.has_left, place.left), (place.has_right, place.right))

    sends = Sends(send, recv)
    for side, (there, device) in enumerate(cols):
        back = cols[1 - side][0]
        sends.add(f"corner{side}", corner_send.at[side], corner_recv.at[1 - side], device, there, back)
        sends.add(f"col{side}", col_send.at[side], col_recv.at[1 - side], device, there, back)
    for side, (there, device) in enumerate(rows):
        back = rows[1 - side][0]
        for name, part in (("m", inner), ("l", outer[0]), ("r", outer[1])):
            sends.add(
                f"row{side}{name}", row_send.at[side, :, :, part], row_recv.at[1 - side, :, :, part],
                device, there, back,
            )

    for c in range(2):
        for r in range(2):
            corner_send[c, r] = acc[:, edges[r], edges[c]].astype(jnp.bfloat16)
        sends.start(f"corner{c}")
    for r in range(2):
        row_send[r, :, :, inner] = acc[:, edges[r], 2 * near:tile].astype(jnp.bfloat16)
        sends.start(f"row{r}m")
    for c in range(2):
        for plane in range(4):
            col_send[c, plane] = acc[plane, own, edges[c]].astype(jnp.bfloat16)
        sends.start(f"col{c}")

    for side in range(2):
        @pl.when(jnp.logical_not(cols[side][0]))
        def _(side=side):
            corner_recv[side] = jnp.zeros(corner_recv.shape[1:], jnp.bfloat16)
            col_recv[side] = jnp.zeros(col_recv.shape[1:], jnp.bfloat16)

        @pl.when(jnp.logical_not(rows[side][0]))
        def _(side=side):
            row_recv[side] = jnp.zeros(row_recv.shape[1:], jnp.bfloat16)

    sends.wait_recv("corner0", "corner1")
    for r in range(2):
        for c, name in enumerate("lr"):
            at = slice(near + outer[c].start, near + outer[c].stop)
            total = acc[:, edges[r], at] + corner_recv[c, r].astype(jnp.float32)
            row_send[r, :, :, outer[c]] = total.astype(jnp.bfloat16)
            sends.start(f"row{r}{name}")

    for plane in range(4):
        out[plane] = acc[plane, own, own]
    sends.wait_recv("col0", "col1")
    for c in range(2):
        for plane in range(4):
            out[plane, :, outer[c]] += col_recv[c, plane].astype(jnp.float32)
    sends.wait_recv("row0m", "row1m", "row0l", "row1l", "row0r", "row1r")
    for r in range(2):
        for plane in range(4):
            out[plane, outer[r], :] += row_recv[r, plane].astype(jnp.float32)
    sends.wait_send()


def margins(acc, tile):
    vmem = pl.BlockSpec(memory_space=pltpu.VMEM)
    row = pltpu.VMEM((2, 4, HALF, tile), jnp.bfloat16)
    col = pltpu.VMEM((2, 4, tile, HALF), jnp.bfloat16)
    corner = pltpu.VMEM((2, 2, 4, HALF, HALF), jnp.bfloat16)
    return pl.pallas_call(
        margin_kernel,
        out_shape=pltpu.VMEM((4, tile, tile), jnp.float32),
        in_specs=[vmem],
        out_specs=vmem,
        scratch_shapes=[
            row, row, col, col, corner, corner,
            pltpu.SemaphoreType.DMA((10,)),
            pltpu.SemaphoreType.DMA((10,)),
        ],
        compiler_params=pltpu.CompilerParams(
            collective_id=1, has_side_effects=True, vmem_limit_bytes=32 * 2**20
        ),
    )(acc)


def output_fold(a, b, first):
    (ca, sa), (cb, sb) = a, b
    if first is None:
        return (ca + sb, cb - sa), (ca - sb, cb + sa)
    sa0, sb0 = jnp.where(first, 0.0, sa), jnp.where(first, 0.0, sb)
    low, high = jnp.where(first, sa, ca), jnp.where(first, sb, cb)
    return (ca + sb0, cb - sa0), (low - sb0, high + sa0)


def input_fold(top, bottom, first):
    (tr, ti), (br, bi) = top, bottom
    if first is None:
        return (tr + br, bi - ti), (ti + bi, tr - br)
    br0, bi0 = jnp.where(first, 0.0, br), jnp.where(first, 0.0, bi)
    return (tr + br0, jnp.where(first, br, bi - ti)), (ti + bi0, jnp.where(first, bi, tr - br))


def times(a, b):
    return a[0] * b[0] - a[1] * b[1], a[0] * b[1] + a[1] * b[0]


def conj_times(a, b):
    return a[0] * b[0] + a[1] * b[1], a[0] * b[1] - a[1] * b[0]


ROWS = 32
FULL = tuple(slice(r, r + ROWS) for r in range(0, EXTENT, ROWS))
UPPER = FULL[: len(FULL) // 2]
LEFT, RIGHT = slice(0, HALF), slice(HALF, EXTENT)


def one_slot(k, live, row, col, light, spread, table, table_t, pick, pick_t, ext, acc, measured,
             field, upper, folded, passed, ordered):
    cols = pl.ds(pl.multiple_of(col * HALF, HALF), EXTENT)
    lane = lax.broadcasted_iota(jnp.int32, (ROWS, HALF), 1) == 0
    top_row = lax.broadcasted_iota(jnp.int32, (ROWS, EXTENT), 0) == 0

    def place(rows):
        return pl.ds(pl.multiple_of(row * HALF + rows.start, ROWS), ROWS)

    def patch(plane, rows):
        at = place(rows)
        return tuple(ext[plane + i, at, cols].astype(jnp.float32) for i in range(2))

    def pair(ref, rows):
        return ref[0, rows, :], ref[1, rows, :]

    def put(ref, rows, value, columns=slice(None)):
        ref[0, rows, columns] = half(value[0])
        ref[1, rows, columns] = half(value[1])

    def add(plane, rows, value):
        at = place(rows)
        for i in range(2):
            acc[plane + i, at, cols] += value[i]

    def wave():
        for rows in FULL:
            put(field, rows, times(pair(light, rows), patch(0, rows)))
        ordered[...] = half(product(pick[...], measured[...]))

    def across():
        a, b = product(field[0], table[...]), product(field[1], table[...])
        for rows in FULL:
            low, high = output_fold(
                (a[rows, LEFT], a[rows, RIGHT]), (b[rows, LEFT], b[rows, RIGHT]), lane
            )
            put(upper, rows, low, LEFT)
            put(upper, rows, high, RIGHT)

    def frequency(act):
        def run():
            a, b = product(table_t[...], upper[0]), product(table_t[...], upper[1])
            for rows in UPPER:
                lower = slice(rows.start + HALF, rows.stop + HALF)
                first = top_row if rows.start == 0 else None
                low, high = output_fold((a[rows], a[lower]), (b[rows], b[lower]), first)
                x, y = input_fold(act(low, rows), act(high, lower), first)
                folded[0, rows, :], folded[0, lower, :] = half(x[0]), half(x[1])
                folded[1, rows, :], folded[1, lower, :] = half(y[0]), half(y[1])
        return run

    def down():
        a, b = product(table[...], folded[0]), product(table[...], folded[1])
        for rows in FULL:
            x, y = input_fold(
                (a[rows, LEFT], b[rows, LEFT]), (a[rows, RIGHT], b[rows, RIGHT]), lane
            )
            upper[0, rows, LEFT], upper[0, rows, RIGHT] = half(x[0]), half(x[1])
            upper[1, rows, LEFT], upper[1, rows, RIGHT] = half(y[0]), half(y[1])

    def space(act):
        def run():
            a, b = product(upper[0], table_t[...]), product(upper[1], table_t[...])
            for rows in FULL:
                act((a[rows], b[rows]), rows)
        return run

    def mix(value, rows):
        return times(pair(spread, rows), value)

    def revert(value, rows):
        return conj_times(pair(spread, rows), value)

    def second(value, rows):
        passed[0, rows, :], passed[1, rows, :] = value
        put(field, rows, times(value, patch(2, rows)))

    def pull():
        intensity = product(ordered[...], pick_t[...])

        def act(value, rows):
            misfit = value[0] * value[0] + value[1] * value[1] - intensity[rows]
            if live is not None:
                misfit = misfit * live
            return misfit * value[0], misfit * value[1]

        frequency(act)()

    def inward(value, rows):
        put(field, rows, conj_times(patch(2, rows), value))
        add(2, rows, conj_times(pair(passed, rows), value))

    def first(value, rows):
        add(0, rows, conj_times(pair(light, rows), value))

    return (
        wave, across, frequency(mix), down, space(second),
        across, pull, down, space(inward),
        across, frequency(revert), down, space(first),
    )


def slot_kernel(
    offsets, count, intensity, light, spread, table, table_t, pick, pick_t, ext, blank, acc,
    measured, field, upper, folded, passed, ordered, sems,
):
    number = count[0]
    steps = lax.div(number + 1, 2)

    def fetch(i, buf):
        return pltpu.make_async_copy(
            intensity.at[pl.ds(2 * i, 2)], measured.at[buf], sems.at[buf]
        )

    @pl.when(steps > 0)
    def _():
        fetch(0, 0).start()

    def one(i, carry):
        buf = lax.rem(i, 2)
        fetch(i, buf).wait()

        @pl.when(i + 1 < steps)
        def _():
            fetch(i + 1, 1 - buf).start()

        live = (2 * i + 1 < number).astype(jnp.float32)
        stages = [
            one_slot(
                k, live if k else None, offsets[0, 2 * i + k] + 1, offsets[1, 2 * i + k] + 1,
                light, spread, table, table_t, pick, pick_t, ext, acc, measured.at[buf, k],
                field.at[k], upper.at[k], folded.at[k], passed.at[k], ordered.at[k],
            )
            for k in range(2)
        ]
        for together in zip(*stages):
            for stage in together:
                stage()
        return carry

    lax.fori_loop(0, steps, one, 0)


def run_slots(offsets, count, intensity, light, spread, constants, ext, acc):
    smem = pl.BlockSpec(memory_space=pltpu.SMEM)
    vmem = pl.BlockSpec(memory_space=pltpu.VMEM)
    return pl.pallas_call(
        slot_kernel,
        out_shape=pltpu.VMEM(ext.shape, jnp.float32),
        in_specs=[smem, smem, pl.BlockSpec(memory_space=pltpu.HBM)] + [vmem] * 8,
        out_specs=vmem,
        scratch_shapes=[
            pltpu.VMEM((2, 2, EXTENT, EXTENT), jnp.bfloat16),
            pltpu.VMEM((2, 2, EXTENT, EXTENT), jnp.bfloat16),
            pltpu.VMEM((2, 2, EXTENT, EXTENT), jnp.bfloat16),
            pltpu.VMEM((2, 2, EXTENT, EXTENT), jnp.bfloat16),
            pltpu.VMEM((2, 2, EXTENT, EXTENT), jnp.float32),
            pltpu.VMEM((2, EXTENT, EXTENT), jnp.bfloat16),
            pltpu.SemaphoreType.DMA((2,)),
        ],
        input_output_aliases={10: 0},
        compiler_params=pltpu.CompilerParams(vmem_limit_bytes=16 * 2**20),
        cost_estimate=pl.CostEstimate(flops=12 * 26 * 2**25, bytes_accessed=2**24, transcendentals=0),
    )(offsets, count, intensity, light, spread, *constants, ext, acc)


def per_device(objects, illumination, propagator_phase, intensity, offsets, counts):
    constants = tables(EXTENT)
    ext, spread, acc = halo(objects, propagator_phase, *constants[2:])
    acc = run_slots(offsets.T, counts, intensity, illumination, spread, constants, ext, acc)
    return margins(acc, objects.shape[1])


def solution(mesh):
    placed = (
        P(None, "row", "col"),
        P(),
        P(),
        P(("row", "col"), None, None),
        P(("row", "col"), None),
        P(("row", "col")),
    )
    return jax.shard_map(
        per_device, mesh=mesh, in_specs=placed, out_specs=P(None, "row", "col"), check_vma=False
    )
```

profile of v0, /device:TPU:20, one launch (start us, length us, event | category | flops | bytes accessed | tf_op | source)
XLA Modules:
  0.0 88.7 jit_solution(11486688947832256139)
XLA Ops:
  0.0 0.0 copy-start
  0.0 0.0 copy-start.4
  0.0 0.0 copy-start.5
  0.0 0.0 copy-start.3
  0.0 0.0 copy-start.1
  0.0 0.0 copy-start.2
  0.8 38.0 %shard_map.100 = (bf16[4,768,768]{2,1,0:T(8,128)(2,1)S(1)}, f32[2,256,256]{2,1,0:T(8,128)S(1)}, f32[4,768,768]{2,1,0:T(8,128)S(1)}) custom-call(f32[4,512,512]{2,1,0:T(8,128)} %objects.1, f32[256,256]{1,0:T(8,128)} %phase.1, bf16[256,256]{1,0:T(8,128)(2,1)} %constant.8.clone.pick.pick_t, bf16[256,256]{1,0:T(8,128)(2,1)} %constant.8.clone.pick.pick_t), custom_call_target="tpu_custom_call" | custom-call | tf_op jit(solution)/shard_map/pallas_call | solution.py:187
  38.9 0.0 copy-done
  38.9 0.0 copy-done.4
  38.9 0.0 copy-done.5
  38.9 0.0 copy-done.3
  38.9 0.0 copy-done.1
  38.9 0.0 copy-done.2
  38.9 16.9 %shard_map.101.acc = f32[4,768,768]{2,1,0:T(8,128)S(1)} custom-call(s32[2,12]{1,0:T(2,128)S(1)} %bitcast.1, s32[1]{0:T(128)S(6)} %copy.15.count, bf16[12,256,256]{2,1,0:T(8,128)(2,1)S(1)} %copy-done.1, f32[2,256,256]{2,1,0:T(8,128)S(1)} %copy-done.2, f32[2,256,256]{2,1,0:T(8,128)S(1)} %get-tuple-element.8.spread, ...), custom_call_target="tpu_custom_call", output_to_operand_aliasing={{}: (10, {})} | custom-call | flops 10468982784 | bytes 16777216 | tf_op jit(solution)/shard_map/pallas_call | solution.py:478
  55.9 30.8 %shard_map.102 = f32[4,512,512]{2,1,0:T(8,128)S(1)} custom-call(f32[4,768,768]{2,1,0:T(8,128)S(1)} %shard_map.101.acc), custom_call_target="tpu_custom_call" | custom-call | tf_op jit(solution)/shard_map/pallas_call | solution.py:285
  86.7 2.0 %copy.14 = f32[4,512,512]{2,1,0:T(8,128)} copy(f32[4,512,512]{2,1,0:T(8,128)S(1)} %shard_map.102) | data formatting | bytes 8388608
Async XLA Ops:
  0.0 38.9 %copy-start = (bf16[256,256]{1,0:T(8,128)(2,1)S(1)}, bf16[256,256]{1,0:T(8,128)(2,1)}, u32[]{:S(2)}) copy-start(bf16[256,256]{1,0:T(8,128)(2,1)} %constant.8.clone.pick.pick_t) | copy-start | bytes 393220
  0.0 38.9 %copy-start.4 = (bf16[256,256]{1,0:T(8,128)(2,1)S(1)}, bf16[256,256]{1,0:T(8,128)(2,1)}, u32[]{:S(2)}) copy-start(bf16[256,256]{1,0:T(8,128)(2,1)} %constant.7.clone.table_t) | copy-start | bytes 393220
  0.0 38.9 %copy-start.5 = (bf16[256,256]{1,0:T(8,128)(2,1)S(1)}, bf16[256,256]{1,0:T(8,128)(2,1)}, u32[]{:S(2)}) copy-start(bf16[256,256]{1,0:T(8,128)(2,1)} %constant.6.clone.table) | copy-start | bytes 393220
  0.0 38.9 %copy-start.3 = (s32[12,2]{0,1:T(2,128)S(1)}, s32[12,2]{0,1:T(2,128)}, u32[]{:S(2)}) copy-start(s32[12,2]{0,1:T(2,128)} %param.14) | copy-start | bytes 292
  0.0 38.9 %copy-start.1 = (bf16[12,256,256]{2,1,0:T(8,128)(2,1)S(1)}, bf16[12,256,256]{2,1,0:T(8,128)(2,1)}, u32[]{:S(2)}) copy-start(bf16[12,256,256]{2,1,0:T(8,128)(2,1)} %intensity.1) | copy-start | bytes 4718596
  0.0 38.9 %copy-start.2 = (f32[2,256,256]{2,1,0:T(8,128)S(1)}, f32[2,256,256]{2,1,0:T(8,128)}, u32[]{:S(2)}) copy-start(f32[2,256,256]{2,1,0:T(8,128)} %light.1) | copy-start | bytes 1572868
where the time goes:
time: 89.7 us; the launch traced here: 88.7 us
  Pallas kernels  85.7 us (96%)
  local copies, waits for them, and re-layouts  2.04 us (2%)
  between operations  0.9 us (1%)
    pallas_call x1, Pallas kernels, halo(): pl.pallas_call(halo_kernel, out_shape=(pltpu.VMEM((4, size, size), jnp.bf...  38 us
    pallas_call x1, Pallas kernels, margins(): pl.pallas_call(margin_kernel, out_shape=pltpu.VMEM((4, tile, tile), jnp.f...  30.8 us
    pallas_call x1, Pallas kernels, run_slots(): pl.pallas_call(slot_kernel, out_shape=pltpu.VMEM(ext.shape, jnp.float32),...  16.9 us
    unnamed x13, local copies, waits for them, and re-layouts  2.04 us

commit v1 on v0

--- a/solution.py
+++ b/solution.py
@@ -35,9 +35,15 @@
     return x.astype(jnp.bfloat16)
 
 
+SEAM = (7, 8)
+RELAYS = ((3, 10), (5, 12))
+PARTNERS = {7: (3, 5), 8: (10, 12), 3: (7, 10), 5: (7, 12), 10: (8, 3), 12: (8, 5)}
+
+
 class Place:
     def __init__(self):
         r, c = lax.axis_index("row"), lax.axis_index("col")
+        self.r, self.c = r, c
         self.has_above, self.has_below = r > 0, r < lax.axis_size("row") - 1
         self.has_left, self.has_right = c > 0, c < lax.axis_size("col") - 1
         self.above, self.below = (r - 1, c), (r + 1, c)
@@ -56,7 +62,15 @@
             def _(device=device):
                 pl.semaphore_signal(barrier, inc=1, device_id=device, device_id_type=MESH)
 
-        pl.semaphore_wait(barrier, sum(there.astype(jnp.int32) for there, _ in self.sides))
+        for column, partners in PARTNERS.items():
+            @pl.when(self.c == column)
+            def _(partners=partners):
+                for other in partners:
+                    pl.semaphore_signal(barrier, inc=1, device_id=(self.r, other), device_id_type=MESH)
+
+        count = sum(there.astype(jnp.int32) for there, _ in self.sides)
+        count = count + 2 * sum((self.c == column).astype(jnp.int32) for column in PARTNERS)
+        pl.semaphore_wait(barrier, count)
 
 
 class Sends:
@@ -81,6 +95,22 @@
             copy, _, received = self.all[key]
             pl.when(received)(copy.wait_recv)
 
+    def relay(self, place, sources, targets, near, far):
+        for g, pair in enumerate(RELAYS):
+            planes = pl.ds(2 * g, 2)
+            for side in range(2):
+                device = tuple((place.r, column) for column in (pair[side], pair[1 - side], SEAM[side]))
+                here = tuple(place.c == column for column in (pair[side], pair[1 - side], SEAM[side]))
+                self.add(f"seam1{g}{side}", sources[side](planes), near, device[0], here[2], here[0])
+                self.add(f"seam2{g}{side}", near, far, device[1], here[0], here[1])
+                self.add(f"seam3{g}{side}", far, targets[side](planes), device[2], here[0], here[2])
+
+    def start_seam(self, step):
+        self.start(*(f"seam{step}{g}{side}" for g in range(2) for side in range(2)))
+
+    def wait_seam(self, step):
+        self.wait_recv(*(f"seam{step}{g}{side}" for g in range(2) for side in range(2)))
+
     def wait_send(self):
         for copy, sent, _ in self.all.values():
             pl.when(sent)(copy.wait_send)
@@ -91,7 +121,8 @@
 
 
 def halo_kernel(
-    objects, phase, pick, pick_t, ext, spread, acc, stage, angle, order, loads, send, recv
+    objects, phase, pick, pick_t, ext, spread, acc, stage, angle, order, near_relay, far_relay,
+    loads, send, recv
 ):
     tile = objects.shape[1]
     near, far, end = HALF, HALF + tile, 2 * HALF + tile
@@ -120,13 +151,29 @@
         sends.add(key, ext.at[(slice(None),) + source], ext.at[(slice(None),) + target], device, sent, received)
 
     middle = slice(2 * near, tile)
-    for name, cols in (("l", top), ("r", bottom), ("m", middle)):
-        route("down" + name, (bottom, cols), (first, cols), place.below, place.has_below, place.has_above)
-        route("up" + name, (top, cols), (last, cols), place.above, place.has_above, place.has_below)
+    every, early, late = slice(None), slice(0, 2), slice(2, 4)
+    for name, planes, cols in (
+        ("l", every, top), ("r", every, bottom), ("m", early, middle), ("n", late, middle)
+    ):
+        for way, source, target, device, sent, received in (
+            ("down", bottom, first, place.below, place.has_below, place.has_above),
+            ("up", top, last, place.above, place.has_above, place.has_below),
+        ):
+            sends.add(way + name, ext.at[planes, source, cols], ext.at[planes, target, cols],
+                      device, sent, received)
     for k, (at, size) in enumerate(bands):
         rows = slice(near + at, near + at + size)
-        route(f"right{k}", (rows, bottom), (rows, first), place.right, place.has_right, place.has_left)
-        route(f"left{k}", (rows, top), (rows, last), place.left, place.has_left, place.has_right)
+        at_left, at_right = place.c != SEAM[0], place.c != SEAM[1]
+        route(f"right{k}", (rows, bottom), (rows, first), place.right,
+              both(place.has_right, at_left), both(place.has_left, at_right))
+        route(f"left{k}", (rows, top), (rows, last), place.left,
+              both(place.has_left, at_right), both(place.has_right, at_left))
+    sends.relay(
+        place,
+        (lambda p: ext.at[p, own, bottom], lambda p: ext.at[p, own, top]),
+        (lambda p: ext.at[p, own, last], lambda p: ext.at[p, own, first]),
+        near_relay, far_relay,
+    )
     for name, rows, there in (("t", first, place.has_above), ("b", last, place.has_below)):
         route("right" + name, (rows, bottom), (rows, first), place.right,
               both(place.has_right, there), both(place.has_left, there))
@@ -144,7 +191,9 @@
     cast(1)
     sends.start("upl", "upr", "right1", "left1")
     cast(2)
-    sends.start("right2", "left2", "downm", "upm")
+    sends.start("right2", "left2")
+    sends.start_seam(1)
+    sends.start("downm", "upm")
 
     def blank(there, rows, cols):
         @pl.when(jnp.logical_not(there))
@@ -159,6 +208,9 @@
     for rows, there in ((first, place.has_above), (last, place.has_below)):
         blank(both(there, place.has_left), rows, first)
         blank(both(there, place.has_right), rows, last)
+    sends.wait_seam(1)
+    sends.start_seam(2)
+    sends.start("downn", "upn")
     for copy in parameters:
         copy.wait()
     rest, ordered = angle[...], 0.0
@@ -175,14 +227,18 @@
     sends.start("leftt", "rightt")
     sends.wait_recv("upl", "upr")
     sends.start("leftb", "rightb")
+    sends.wait_seam(2)
+    sends.start_seam(3)
     sends.wait_recv(*(f"{side}{k}" for side in ("right", "left") for k in range(3)))
-    sends.wait_recv("downm", "upm", "leftt", "rightt", "leftb", "rightb")
+    sends.wait_seam(3)
+    sends.wait_recv("downn", "upn", "downm", "upm", "leftt", "rightt", "leftb", "rightb")
     sends.wait_send()
 
 
 def halo(objects, phase, pick, pick_t):
     tile = objects.shape[1]
     size = tile + 2 * HALF
+    relay = pltpu.VMEM((2, tile, HALF), jnp.bfloat16)
     vmem = pl.BlockSpec(memory_space=pltpu.VMEM)
     return pl.pallas_call(
         halo_kernel,
@@ -197,9 +253,11 @@
             pltpu.VMEM(objects.shape, jnp.float32),
             pltpu.VMEM((EXTENT, EXTENT), jnp.float32),
             pltpu.VMEM((2, EXTENT, EXTENT), jnp.bfloat16),
+            relay,
+            relay,
             pltpu.SemaphoreType.DMA((6,)),
-            pltpu.SemaphoreType.DMA((16,)),
-            pltpu.SemaphoreType.DMA((16,)),
+            pltpu.SemaphoreType.DMA((30,)),
+            pltpu.SemaphoreType.DMA((30,)),
         ],
         compiler_params=pltpu.CompilerParams(
             collective_id=0, has_side_effects=True, vmem_limit_bytes=24 * 2**20
@@ -208,7 +266,8 @@
 
 
 def margin_kernel(
-    acc, out, row_send, row_recv, col_send, col_recv, corner_send, corner_recv, send, recv
+    acc, out, row_send, row_recv, col_send, col_recv, corner_send, corner_recv,
+    near_relay, far_relay, send, recv
 ):
     tile = out.shape[1]
     near, far, end = HALF, HALF + tile, 2 * HALF + tile
@@ -225,7 +284,14 @@
     for side, (there, device) in enumerate(cols):
         back = cols[1 - side][0]
         sends.add(f"corner{side}", corner_send.at[side], corner_recv.at[1 - side], device, there, back)
-        sends.add(f"col{side}", col_send.at[side], col_recv.at[1 - side], device, there, back)
+        sends.add(f"col{side}", col_send.at[side], col_recv.at[1 - side], device,
+                  both(there, place.c != SEAM[1 - side]), both(back, place.c != SEAM[side]))
+    sends.relay(
+        place,
+        (lambda p: col_send.at[1, p], lambda p: col_send.at[0, p]),
+        (lambda p: col_recv.at[1, p], lambda p: col_recv.at[0, p]),
+        near_relay, far_relay,
+    )
     for side, (there, device) in enumerate(rows):
         back = rows[1 - side][0]
         for name, part in (("m", inner), ("l", outer[0]), ("r", outer[1])):
@@ -245,6 +311,7 @@
         for plane in range(4):
             col_send[c, plane] = acc[plane, own, edges[c]].astype(jnp.bfloat16)
         sends.start(f"col{c}")
+    sends.start_seam(1)
 
     for side in range(2):
         @pl.when(jnp.logical_not(cols[side][0]))
@@ -256,6 +323,8 @@
         def _(side=side):
             row_recv[side] = jnp.zeros(row_recv.shape[1:], jnp.bfloat16)
 
+    sends.wait_seam(1)
+    sends.start_seam(2)
     sends.wait_recv("corner0", "corner1")
     for r in range(2):
         for c, name in enumerate("lr"):
@@ -266,7 +335,10 @@
 
     for plane in range(4):
         out[plane] = acc[plane, own, own]
+    sends.wait_seam(2)
+    sends.start_seam(3)
     sends.wait_recv("col0", "col1")
+    sends.wait_seam(3)
     for c in range(2):
         for plane in range(4):
             out[plane, :, outer[c]] += col_recv[c, plane].astype(jnp.float32)
@@ -281,6 +353,7 @@
     vmem = pl.BlockSpec(memory_space=pltpu.VMEM)
     row = pltpu.VMEM((2, 4, HALF, tile), jnp.bfloat16)
     col = pltpu.VMEM((2, 4, tile, HALF), jnp.bfloat16)
+    relay = pltpu.VMEM((2, tile, HALF), jnp.bfloat16)
     corner = pltpu.VMEM((2, 2, 4, HALF, HALF), jnp.bfloat16)
     return pl.pallas_call(
         margin_kernel,
@@ -288,9 +361,9 @@
         in_specs=[vmem],
         out_specs=vmem,
         scratch_shapes=[
-            row, row, col, col, corner, corner,
-            pltpu.SemaphoreType.DMA((10,)),
-            pltpu.SemaphoreType.DMA((10,)),
+            row, row, col, col, corner, corner, relay, relay,
+            pltpu.SemaphoreType.DMA((22,)),
+            pltpu.SemaphoreType.DMA((22,)),
         ],
         compiler_params=pltpu.CompilerParams(
             collective_id=1, has_side_effects=True, vmem_limit_bytes=32 * 2**20

time: 89.7 us -> 86 us (0.959)
  the two profiles are of different devices: /device:TPU:20 before, /device:TPU:28 now
where the time goes in v1:
time: 86 us; the launch traced here: 85.9 us
  Pallas kernels  83 us (97%)
  local copies, waits for them, and re-layouts  2.04 us (2%)
  between operations  0.9 us (1%)
    pallas_call x1, Pallas kernels, halo(): pl.pallas_call(halo_kernel, out_shape=(pltpu.VMEM((4, size, size), jnp.bf...  37 us
    pallas_call x1, Pallas kernels, margins(): pl.pallas_call(margin_kernel, out_shape=pltpu.VMEM((4, tile, tile), jnp.f...  29.1 us
    pallas_call x1, Pallas kernels, run_slots(): pl.pallas_call(slot_kernel, out_shape=pltpu.VMEM(ext.shape, jnp.float32),...  16.9 us
    unnamed x13, local copies, waits for them, and re-layouts  2.04 us

profile of v1, /device:TPU:28, one launch (start us, length us, event | category | flops | bytes accessed | tf_op | source)
XLA Modules:
  0.0 85.9 jit_solution(12178067678967085721)
XLA Ops:
  0.0 0.0 copy-start
  0.0 0.0 copy-start.4
  0.0 0.0 copy-start.5
  0.0 0.0 copy-start.3
  0.0 0.0 copy-start.1
  0.0 0.0 copy-start.2
  0.8 37.0 %shard_map.100 = (bf16[4,768,768]{2,1,0:T(8,128)(2,1)S(1)}, f32[2,256,256]{2,1,0:T(8,128)S(1)}, f32[4,768,768]{2,1,0:T(8,128)S(1)}) custom-call(f32[4,512,512]{2,1,0:T(8,128)} %objects.1, f32[256,256]{1,0:T(8,128)} %phase.1, bf16[256,256]{1,0:T(8,128)(2,1)} %constant.8.clone.pick.pick_t, bf16[256,256]{1,0:T(8,128)(2,1)} %constant.8.clone.pick.pick_t), custom_call_target="tpu_custom_call" | custom-call | tf_op jit(solution)/shard_map/pallas_call | solution.py:243
  37.8 0.0 copy-done
  37.9 0.0 copy-done.4
  37.9 0.0 copy-done.5
  37.9 0.0 copy-done.3
  37.9 0.0 copy-done.1
  37.9 0.0 copy-done.2
  37.9 16.9 %shard_map.101.acc = f32[4,768,768]{2,1,0:T(8,128)S(1)} custom-call(s32[2,12]{1,0:T(2,128)S(1)} %bitcast.1, s32[1]{0:T(128)S(6)} %copy.15.count, bf16[12,256,256]{2,1,0:T(8,128)(2,1)S(1)} %copy-done.1, f32[2,256,256]{2,1,0:T(8,128)S(1)} %copy-done.2, f32[2,256,256]{2,1,0:T(8,128)S(1)} %get-tuple-element.8.spread, ...), custom_call_target="tpu_custom_call", output_to_operand_aliasing={{}: (10, {})} | custom-call | flops 10468982784 | bytes 16777216 | tf_op jit(solution)/shard_map/pallas_call | solution.py:551
  54.8 29.1 %shard_map.102 = f32[4,512,512]{2,1,0:T(8,128)S(1)} custom-call(f32[4,768,768]{2,1,0:T(8,128)S(1)} %shard_map.101.acc), custom_call_target="tpu_custom_call" | custom-call | tf_op jit(solution)/shard_map/pallas_call | solution.py:358
  83.9 2.0 %copy.14 = f32[4,512,512]{2,1,0:T(8,128)} copy(f32[4,512,512]{2,1,0:T(8,128)S(1)} %shard_map.102) | data formatting | bytes 8388608
Async XLA Ops:
  0.0 37.9 %copy-start = (bf16[256,256]{1,0:T(8,128)(2,1)S(1)}, bf16[256,256]{1,0:T(8,128)(2,1)}, u32[]{:S(2)}) copy-start(bf16[256,256]{1,0:T(8,128)(2,1)} %constant.8.clone.pick.pick_t) | copy-start | bytes 393220
  0.0 37.9 %copy-start.4 = (bf16[256,256]{1,0:T(8,128)(2,1)S(1)}, bf16[256,256]{1,0:T(8,128)(2,1)}, u32[]{:S(2)}) copy-start(bf16[256,256]{1,0:T(8,128)(2,1)} %constant.7.clone.table_t) | copy-start | bytes 393220
  0.0 37.9 %copy-start.5 = (bf16[256,256]{1,0:T(8,128)(2,1)S(1)}, bf16[256,256]{1,0:T(8,128)(2,1)}, u32[]{:S(2)}) copy-start(bf16[256,256]{1,0:T(8,128)(2,1)} %constant.6.clone.table) | copy-start | bytes 393220
  0.0 37.9 %copy-start.3 = (s32[12,2]{0,1:T(2,128)S(1)}, s32[12,2]{0,1:T(2,128)}, u32[]{:S(2)}) copy-start(s32[12,2]{0,1:T(2,128)} %param.14) | copy-start | bytes 292
  0.0 37.9 %copy-start.1 = (bf16[12,256,256]{2,1,0:T(8,128)(2,1)S(1)}, bf16[12,256,256]{2,1,0:T(8,128)(2,1)}, u32[]{:S(2)}) copy-start(bf16[12,256,256]{2,1,0:T(8,128)(2,1)} %intensity.1) | copy-start | bytes 4718596
  0.0 37.9 %copy-start.2 = (f32[2,256,256]{2,1,0:T(8,128)S(1)}, f32[2,256,256]{2,1,0:T(8,128)}, u32[]{:S(2)}) copy-start(f32[2,256,256]{2,1,0:T(8,128)} %light.1) | copy-start | bytes 1572868

commit v2 on v1

--- a/solution.py
+++ b/solution.py
@@ -208,9 +208,6 @@
     for rows, there in ((first, place.has_above), (last, place.has_below)):
         blank(both(there, place.has_left), rows, first)
         blank(both(there, place.has_right), rows, last)
-    sends.wait_seam(1)
-    sends.start_seam(2)
-    sends.start("downn", "upn")
     for copy in parameters:
         copy.wait()
     rest, ordered = angle[...], 0.0
@@ -223,10 +220,13 @@
     for plane in range(4):
         acc[plane] = jnp.zeros(acc.shape[1:], jnp.float32)
 
+    sends.wait_seam(1)
+    sends.start_seam(2)
     sends.wait_recv("downl", "downr")
     sends.start("leftt", "rightt")
     sends.wait_recv("upl", "upr")
     sends.start("leftb", "rightb")
+    sends.start("downn", "upn")
     sends.wait_seam(2)
     sends.start_seam(3)
     sends.wait_recv(*(f"{side}{k}" for side in ("right", "left") for k in range(3)))
@@ -304,14 +304,14 @@
         for r in range(2):
             corner_send[c, r] = acc[:, edges[r], edges[c]].astype(jnp.bfloat16)
         sends.start(f"corner{c}")
+    for c in range(2):
+        for plane in range(4):
+            col_send[c, plane] = acc[plane, own, edges[c]].astype(jnp.bfloat16)
+    sends.start_seam(1)
     for r in range(2):
         row_send[r, :, :, inner] = acc[:, edges[r], 2 * near:tile].astype(jnp.bfloat16)
         sends.start(f"row{r}m")
-    for c in range(2):
-        for plane in range(4):
-            col_send[c, plane] = acc[plane, own, edges[c]].astype(jnp.bfloat16)
-        sends.start(f"col{c}")
-    sends.start_seam(1)
+    sends.start("col0", "col1")
 
     for side in range(2):
         @pl.when(jnp.logical_not(cols[side][0]))
@@ -323,11 +323,12 @@
         def _(side=side):
             row_recv[side] = jnp.zeros(row_recv.shape[1:], jnp.bfloat16)
 
-    sends.wait_seam(1)
-    sends.start_seam(2)
     sends.wait_recv("corner0", "corner1")
-    for r in range(2):
-        for c, name in enumerate("lr"):
+    for c, name in enumerate("lr"):
+        if c == 1:
+            sends.wait_seam(1)
+            sends.start_seam(2)
+        for r in range(2):
             at = slice(near + outer[c].start, near + outer[c].stop)
             total = acc[:, edges[r], at] + corner_recv[c, r].astype(jnp.float32)
             row_send[r, :, :, outer[c]] = total.astype(jnp.bfloat16)

time: 86 us -> 87.5 us (1.017)
  the two profiles are of different devices: /device:TPU:28 before, /device:TPU:30 now
where the time goes in v2:
time: 87.5 us; the launch traced here: 86.4 us
  Pallas kernels  83.5 us (95%)
  local copies, waits for them, and re-layouts  2.04 us (2%)
  between operations  0.9 us (1%)
    pallas_call x1, Pallas kernels, margins(): pl.pallas_call(margin_kernel, out_shape=pltpu.VMEM((4, tile, tile), jnp.f...  39.3 us
    pallas_call x1, Pallas kernels, halo(): pl.pallas_call(halo_kernel, out_shape=(pltpu.VMEM((4, size, size), jnp.bf...  37.1 us
    pallas_call x1, Pallas kernels, run_slots(): pl.pallas_call(slot_kernel, out_shape=pltpu.VMEM(ext.shape, jnp.float32),...  7.08 us
    unnamed x13, local copies, waits for them, and re-layouts  2.04 us

profile of v2, /device:TPU:30, one launch (start us, length us, event | category | flops | bytes accessed | tf_op | source)
XLA Modules:
  0.0 86.4 jit_solution(6806590649038684987)
XLA Ops:
  0.0 0.0 copy-start
  0.0 0.0 copy-start.4
  0.0 0.0 copy-start.5
  0.0 0.0 copy-start.3
  0.0 0.0 copy-start.1
  0.0 0.0 copy-start.2
  0.8 37.1 %shard_map.100 = (bf16[4,768,768]{2,1,0:T(8,128)(2,1)S(1)}, f32[2,256,256]{2,1,0:T(8,128)S(1)}, f32[4,768,768]{2,1,0:T(8,128)S(1)}) custom-call(f32[4,512,512]{2,1,0:T(8,128)} %objects.1, f32[256,256]{1,0:T(8,128)} %phase.1, bf16[256,256]{1,0:T(8,128)(2,1)} %constant.8.clone.pick.pick_t, bf16[256,256]{1,0:T(8,128)(2,1)} %constant.8.clone.pick.pick_t), custom_call_target="tpu_custom_call" | custom-call | tf_op jit(solution)/shard_map/pallas_call | solution.py:243
  38.0 0.0 copy-done
  38.0 0.0 copy-done.4
  38.0 0.0 copy-done.5
  38.0 0.0 copy-done.3
  38.0 0.0 copy-done.1
  38.0 0.0 copy-done.2
  38.0 7.1 %shard_map.101.acc = f32[4,768,768]{2,1,0:T(8,128)S(1)} custom-call(s32[2,12]{1,0:T(2,128)S(1)} %bitcast.1, s32[1]{0:T(128)S(6)} %copy.15.count, bf16[12,256,256]{2,1,0:T(8,128)(2,1)S(1)} %copy-done.1, f32[2,256,256]{2,1,0:T(8,128)S(1)} %copy-done.2, f32[2,256,256]{2,1,0:T(8,128)S(1)} %get-tuple-element.8.spread, ...), custom_call_target="tpu_custom_call", output_to_operand_aliasing={{}: (10, {})} | custom-call | flops 10468982784 | bytes 16777216 | tf_op jit(solution)/shard_map/pallas_call | solution.py:552
  45.1 39.3 %shard_map.102 = f32[4,512,512]{2,1,0:T(8,128)S(1)} custom-call(f32[4,768,768]{2,1,0:T(8,128)S(1)} %shard_map.101.acc), custom_call_target="tpu_custom_call" | custom-call | tf_op jit(solution)/shard_map/pallas_call | solution.py:359
  84.4 2.0 %copy.14 = f32[4,512,512]{2,1,0:T(8,128)} copy(f32[4,512,512]{2,1,0:T(8,128)S(1)} %shard_map.102) | data formatting | bytes 8388608
Async XLA Ops:
  0.0 38.0 %copy-start = (bf16[256,256]{1,0:T(8,128)(2,1)S(1)}, bf16[256,256]{1,0:T(8,128)(2,1)}, u32[]{:S(2)}) copy-start(bf16[256,256]{1,0:T(8,128)(2,1)} %constant.8.clone.pick.pick_t) | copy-start | bytes 393220
  0.0 38.0 %copy-start.4 = (bf16[256,256]{1,0:T(8,128)(2,1)S(1)}, bf16[256,256]{1,0:T(8,128)(2,1)}, u32[]{:S(2)}) copy-start(bf16[256,256]{1,0:T(8,128)(2,1)} %constant.7.clone.table_t) | copy-start | bytes 393220
  0.0 38.0 %copy-start.5 = (bf16[256,256]{1,0:T(8,128)(2,1)S(1)}, bf16[256,256]{1,0:T(8,128)(2,1)}, u32[]{:S(2)}) copy-start(bf16[256,256]{1,0:T(8,128)(2,1)} %constant.6.clone.table) | copy-start | bytes 393220
  0.0 38.0 %copy-start.3 = (s32[12,2]{0,1:T(2,128)S(1)}, s32[12,2]{0,1:T(2,128)}, u32[]{:S(2)}) copy-start(s32[12,2]{0,1:T(2,128)} %param.14) | copy-start | bytes 292
  0.0 38.0 %copy-start.1 = (bf16[12,256,256]{2,1,0:T(8,128)(2,1)S(1)}, bf16[12,256,256]{2,1,0:T(8,128)(2,1)}, u32[]{:S(2)}) copy-start(bf16[12,256,256]{2,1,0:T(8,128)(2,1)} %intensity.1) | copy-start | bytes 4718596
  0.0 38.0 %copy-start.2 = (f32[2,256,256]{2,1,0:T(8,128)S(1)}, f32[2,256,256]{2,1,0:T(8,128)}, u32[]{:S(2)}) copy-start(f32[2,256,256]{2,1,0:T(8,128)} %light.1) | copy-start | bytes 1572868

commit v3 on v2

--- a/solution.py
+++ b/solution.py
@@ -96,8 +96,12 @@
             pl.when(received)(copy.wait_recv)
 
     def relay(self, place, sources, targets, near, far):
+        rest = pl.ds(2, 2)
+        for side in range(2):
+            self.add(f"seam{side}", sources[side](rest), targets[1 - side](rest),
+                     (place.r, SEAM[1 - side]), place.c == SEAM[side], place.c == SEAM[1 - side])
         for g, pair in enumerate(RELAYS):
-            planes = pl.ds(2 * g, 2)
+            planes = pl.ds(g, 1)
             for side in range(2):
                 device = tuple((place.r, column) for column in (pair[side], pair[1 - side], SEAM[side]))
                 here = tuple(place.c == column for column in (pair[side], pair[1 - side], SEAM[side]))
@@ -107,9 +111,13 @@
 
     def start_seam(self, step):
         self.start(*(f"seam{step}{g}{side}" for g in range(2) for side in range(2)))
+        if step == 1:
+            self.start("seam0", "seam1")
 
     def wait_seam(self, step):
         self.wait_recv(*(f"seam{step}{g}{side}" for g in range(2) for side in range(2)))
+        if step == 3:
+            self.wait_recv("seam0", "seam1")
 
     def wait_send(self):
         for copy, sent, _ in self.all.values():
@@ -238,7 +246,7 @@
 def halo(objects, phase, pick, pick_t):
     tile = objects.shape[1]
     size = tile + 2 * HALF
-    relay = pltpu.VMEM((2, tile, HALF), jnp.bfloat16)
+    relay = pltpu.VMEM((1, tile, HALF), jnp.bfloat16)
     vmem = pl.BlockSpec(memory_space=pltpu.VMEM)
     return pl.pallas_call(
         halo_kernel,
@@ -256,8 +264,8 @@
             relay,
             relay,
             pltpu.SemaphoreType.DMA((6,)),
-            pltpu.SemaphoreType.DMA((30,)),
-            pltpu.SemaphoreType.DMA((30,)),
+            pltpu.SemaphoreType.DMA((32,)),
+            pltpu.SemaphoreType.DMA((32,)),
         ],
         compiler_params=pltpu.CompilerParams(
             collective_id=0, has_side_effects=True, vmem_limit_bytes=24 * 2**20
@@ -354,7 +362,7 @@
     vmem = pl.BlockSpec(memory_space=pltpu.VMEM)
     row = pltpu.VMEM((2, 4, HALF, tile), jnp.bfloat16)
     col = pltpu.VMEM((2, 4, tile, HALF), jnp.bfloat16)
-    relay = pltpu.VMEM((2, tile, HALF), jnp.bfloat16)
+    relay = pltpu.VMEM((1, tile, HALF), jnp.bfloat16)
     corner = pltpu.VMEM((2, 2, 4, HALF, HALF), jnp.bfloat16)
     return pl.pallas_call(
         margin_kernel,
@@ -363,8 +371,8 @@
         out_specs=vmem,
         scratch_shapes=[
             row, row, col, col, corner, corner, relay, relay,
-            pltpu.SemaphoreType.DMA((22,)),
-            pltpu.SemaphoreType.DMA((22,)),
+            pltpu.SemaphoreType.DMA((24,)),
+            pltpu.SemaphoreType.DMA((24,)),
         ],
         compiler_params=pltpu.CompilerParams(
             collective_id=1, has_side_effects=True, vmem_limit_bytes=32 * 2**20

time: 87.5 us -> 82.4 us (0.942)
  the two profiles are of different devices: /device:TPU:30 before, /device:TPU:20 now
where the time goes in v3:
time: 82.4 us; the launch traced here: 82.5 us
  Pallas kernels  79.6 us (97%)
  local copies, waits for them, and re-layouts  2.04 us (2%)
  between operations  0.9 us (1%)
    pallas_call x1, Pallas kernels, halo(): pl.pallas_call(halo_kernel, out_shape=(pltpu.VMEM((4, size, size), jnp.bf...  35.5 us
    pallas_call x1, Pallas kernels, margins(): pl.pallas_call(margin_kernel, out_shape=pltpu.VMEM((4, tile, tile), jnp.f...  33.7 us
    pallas_call x1, Pallas kernels, run_slots(): pl.pallas_call(slot_kernel, out_shape=pltpu.VMEM(ext.shape, jnp.float32),...  10.4 us
    unnamed x13, local copies, waits for them, and re-layouts  2.04 us

profile of v3, /device:TPU:20, one launch (start us, length us, event | category | flops | bytes accessed | tf_op | source)
XLA Modules:
  0.0 82.5 jit_solution(16091236056976569363)
XLA Ops:
  0.0 0.0 copy-start
  0.0 0.0 copy-start.4
  0.0 0.0 copy-start.5
  0.0 0.0 copy-start.3
  0.0 0.0 copy-start.1
  0.0 0.0 copy-start.2
  0.8 35.5 %shard_map.100 = (bf16[4,768,768]{2,1,0:T(8,128)(2,1)S(1)}, f32[2,256,256]{2,1,0:T(8,128)S(1)}, f32[4,768,768]{2,1,0:T(8,128)S(1)}) custom-call(f32[4,512,512]{2,1,0:T(8,128)} %objects.1, f32[256,256]{1,0:T(8,128)} %phase.1, bf16[256,256]{1,0:T(8,128)(2,1)} %constant.8.clone.pick.pick_t, bf16[256,256]{1,0:T(8,128)(2,1)} %constant.8.clone.pick.pick_t), custom_call_target="tpu_custom_call" | custom-call | tf_op jit(solution)/shard_map/pallas_call | solution.py:251
  36.4 0.0 copy-done
  36.4 0.0 copy-done.4
  36.4 0.0 copy-done.5
  36.4 0.0 copy-done.3
  36.4 0.0 copy-done.1
  36.4 0.0 copy-done.2
  36.4 10.4 %shard_map.101.acc = f32[4,768,768]{2,1,0:T(8,128)S(1)} custom-call(s32[2,12]{1,0:T(2,128)S(1)} %bitcast.1, s32[1]{0:T(128)S(6)} %copy.15.count, bf16[12,256,256]{2,1,0:T(8,128)(2,1)S(1)} %copy-done.1, f32[2,256,256]{2,1,0:T(8,128)S(1)} %copy-done.2, f32[2,256,256]{2,1,0:T(8,128)S(1)} %get-tuple-element.8.spread, ...), custom_call_target="tpu_custom_call", output_to_operand_aliasing={{}: (10, {})} | custom-call | flops 10468982784 | bytes 16777216 | tf_op jit(solution)/shard_map/pallas_call | solution.py:560
  46.8 33.7 %shard_map.102 = f32[4,512,512]{2,1,0:T(8,128)S(1)} custom-call(f32[4,768,768]{2,1,0:T(8,128)S(1)} %shard_map.101.acc), custom_call_target="tpu_custom_call" | custom-call | tf_op jit(solution)/shard_map/pallas_call | solution.py:367
  80.5 2.0 %copy.14 = f32[4,512,512]{2,1,0:T(8,128)} copy(f32[4,512,512]{2,1,0:T(8,128)S(1)} %shard_map.102) | data formatting | bytes 8388608
Async XLA Ops:
  0.0 36.4 %copy-start = (bf16[256,256]{1,0:T(8,128)(2,1)S(1)}, bf16[256,256]{1,0:T(8,128)(2,1)}, u32[]{:S(2)}) copy-start(bf16[256,256]{1,0:T(8,128)(2,1)} %constant.8.clone.pick.pick_t) | copy-start | bytes 393220
  0.0 36.4 %copy-start.4 = (bf16[256,256]{1,0:T(8,128)(2,1)S(1)}, bf16[256,256]{1,0:T(8,128)(2,1)}, u32[]{:S(2)}) copy-start(bf16[256,256]{1,0:T(8,128)(2,1)} %constant.7.clone.table_t) | copy-start | bytes 393220
  0.0 36.4 %copy-start.5 = (bf16[256,256]{1,0:T(8,128)(2,1)S(1)}, bf16[256,256]{1,0:T(8,128)(2,1)}, u32[]{:S(2)}) copy-start(bf16[256,256]{1,0:T(8,128)(2,1)} %constant.6.clone.table) | copy-start | bytes 393220
  0.0 36.4 %copy-start.3 = (s32[12,2]{0,1:T(2,128)S(1)}, s32[12,2]{0,1:T(2,128)}, u32[]{:S(2)}) copy-start(s32[12,2]{0,1:T(2,128)} %param.14) | copy-start | bytes 292
  0.0 36.4 %copy-start.1 = (bf16[12,256,256]{2,1,0:T(8,128)(2,1)S(1)}, bf16[12,256,256]{2,1,0:T(8,128)(2,1)}, u32[]{:S(2)}) copy-start(bf16[12,256,256]{2,1,0:T(8,128)(2,1)} %intensity.1) | copy-start | bytes 4718596
  0.0 36.4 %copy-start.2 = (f32[2,256,256]{2,1,0:T(8,128)S(1)}, f32[2,256,256]{2,1,0:T(8,128)}, u32[]{:S(2)}) copy-start(f32[2,256,256]{2,1,0:T(8,128)} %light.1) | copy-start | bytes 1572868
